TPU v7x, 16 devices: a 4x2x1 block of a 4x4x8 slice. The times are simulated.
16 devices in a mesh: rep: 2 (over y, z), dp: 8 (over x, core).
Axes of the slice: x: 4, y: 2, z: 1, core: 2. Of those that a mesh axis runs over, the one named last changes fastest.
The devices are a block of a 4x4x8 slice.
Arguments:
- x: bfloat16 [16, 2048, 768], P(('rep', 'dp')), parts along dimension 0
- dy: bfloat16 [16, 2048, 768], P(('rep', 'dp')), parts along dimension 0
- w_gate: bfloat16 [2, 768, 1792], replicated
- w_up: bfloat16 [2, 768, 1792], replicated
- w_down: bfloat16 [2, 1792, 768], replicated
- m_w_gate: float32 [2, 768, 1792], replicated
- m_w_up: float32 [2, 768, 1792], replicated
- m_w_down: float32 [2, 1792, 768], replicated
- v_w_gate: float32 [2, 768, 1792], replicated
- v_w_up: float32 [2, 768, 1792], replicated
- v_w_down: float32 [2, 1792, 768], replicated
Outputs:
- output 1: bfloat16 [4, 768, 1792], P('rep'), parts along dimension 0
- output 2: bfloat16 [4, 768, 1792], P('rep'), parts along dimension 0
- output 3: bfloat16 [4, 1792, 768], P('rep'), parts along dimension 0
- output 4: float32 [4, 768, 1792], P('rep'), parts along dimension 0
- output 5: float32 [4, 768, 1792], P('rep'), parts along dimension 0
- output 6: float32 [4, 1792, 768], P('rep'), parts along dimension 0
- output 7: float32 [4, 768, 1792], P('rep'), parts along dimension 0
- output 8: float32 [4, 768, 1792], P('rep'), parts along dimension 0
- output 9: float32 [4, 1792, 768], P('rep'), parts along dimension 0
There are 2 independent parts. A program takes and returns all parts, laid end to end along the dimension named above; an argument that names none is the same for every part.
All inputs are finite; a program needn't handle non-finite values.
Results may differ from a plain program's by a relative error of at most 0.022.
Values are sent between devices in bfloat16 or wider.
A program may use at most 768 MiB of HBM per device.

v0:
```python
import jax
import jax.numpy as jnp
from jax import lax
from jax.sharding import PartitionSpec as P

NAMES = ("w_gate", "w_up", "w_down")


def matmul(a, w):
    return jnp.dot(a, w, preferred_element_type=jnp.float32).astype(jnp.bfloat16)


def normed(h):
    wide = h.astype(jnp.float32)
    scale = lax.rsqrt(jnp.mean(wide**2, -1, keepdims=True) + 1e-6)
    return (wide * scale).astype(jnp.bfloat16)


def layer(h, w):
    a = normed(h)
    gate = jnp.dot(a, w["w_gate"], preferred_element_type=jnp.float32)
    up = jnp.dot(a, w["w_up"], preferred_element_type=jnp.float32)
    return h + matmul((jax.nn.silu(gate) * up).astype(jnp.bfloat16), w["w_down"])


def adamw(w, m, v, g):
    m = 0.9 * m + 0.1 * g
    v = 0.95 * v + 0.05 * g * g
    step = m * lax.rsqrt(v + 1e-8) + 0.1 * w
    return (w - 0.02 * step).astype(jnp.bfloat16), m, v


def clipped(gradients, sum_of_squares, count):
    factor = jnp.minimum(1.0, 0.5 * lax.rsqrt(sum_of_squares / count + 1e-30))
    return [g * factor for g in gradients]


def solution(mesh):
    def step(x, dy, *arrays):
        weights, m, v = (arrays[i : i + 3] for i in (0, 3, 6))
        layers = weights[0].shape[0]
        h, kept = x[0], []
        for number in range(layers):
            kept.append(h)
            h = layer(h, {name: w[number] for name, w in zip(NAMES, weights, strict=True)})
        by_h, summed = dy[0], [None] * layers
        for number in reversed(range(layers)):
            _, back = jax.vjp(lambda w, h: layer(h, w), {name: w[number] for name, w in zip(NAMES, weights, strict=True)}, kept[number])
            by_w, by_h = back(by_h)
            summed[number] = [lax.psum(by_w[name], "dp") for name in NAMES]
        gradients = [jnp.stack([summed[number][i] for number in range(layers)]).astype(jnp.float32) for i in range(3)]
        gradients = clipped(gradients, sum(jnp.sum(g * g) for g in gradients), sum(g.size for g in gradients))
        new = [adamw(w.astype(jnp.float32), m, v, g) for w, m, v, g in zip(weights, m, v, gradients, strict=True)]
        return tuple(one[which] for which in range(3) for one in new)

    return jax.shard_map(
        step,
        mesh=mesh,
        in_specs=(P(("rep", "dp"), None, None),) * 2 + (P(None, None, None),) * 9,
        out_specs=(P("rep", None, None),) * 9,
        check_vma=False,
    )
```

profile of v0, /device:TPU:113, one launch (start us, length us, event | category | flops | bytes accessed | tf_op | source)
XLA Modules:
  0.0 469.9 jit_solution(13721173598129994024)
XLA Ops:
  7.2 0.1 all-reduce.3.cloned.1.call-start
  7.3 3.2 copy.20
  10.5 0.0 copy-start
  10.5 0.7 fusion.36
  11.1 0.0 copy-start.12
  11.2 5.0 %copy.21 = bf16[1,2048,768]{1,2,0:T(8,128)(2,1)} copy(bf16[1,2048,768]{2,1,0:T(8,128)(2,1)} %param.12) | data formatting | bytes 6291456 | tf_op args[1]
  16.2 0.0 copy-start.5
  16.2 0.0 slice-start
  16.2 10.4 %convolution_convert_fusion.1 = bf16[2048,1792]{1,0:T(8,128)(2,1)} fusion(bf16[1,2048,768]{2,1,0:T(8,128)(2,1)} %param.12, bf16[2,1792,768]{2,1,0:T(8,128)(2,1)} %param.15), kind=kOutput, calls=%fused_computation.66 | convolution fusion | flops 5640814592 | bytes 13238272 | tf_op jit(solution)/shard_map/transpose(jvp())/dot_general | solution.py:10
  26.5 0.0 copy-done.5
  26.5 0.0 slice-start.1
  26.5 11.1 %fusion.77 = f32[2048,1792]{1,0:T(8,128)} fusion(bf16[2,768,1792]{2,1,0:T(8,128)(2,1)} %param.13, bf16[1,2048,768]{2,1,0:T(8,128)(2,1)S(1)} %copy-done.5, f32[2048]{0:T(1024)S(1)} %add_rsqrt_fusion), kind=kOutput, calls=%fused_computation.111 | convolution fusion | flops 5641863168 | bytes 20586496 | tf_op jit(solution)/shard_map/dot_general | solution.py:21
  37.6 0.0 copy-done.12
  37.6 0.0 slice-done
  37.6 0.0 slice-done.1
  37.6 16.2 %multiply_convert_fusion.1 = (bf16[2048,1792]{1,0:T(8,128)(2,1)}, f32[2048,1792]{1,0:T(8,128)}) fusion(f32[2048,1792]{1,0:T(8,128)} %fusion.77, bf16[2,768,1792]{2,1,0:T(8,128)(2,1)S(1)} %bitcast.77, bf16[1,2048,768]{2,1,0:T(8,128)(2,1)} %param.11, f32[2048]{0:T(1024)S(1)} %add_rsqrt_fusion), kind=kOutput, calls=%fused_computation.20 | convolution fusion | flops 5663883264 | bytes 42606592 | tf_op jit(solution)/shard_map/dot_general | solution.py:22
  53.9 0.0 copy-done
  53.9 9.7 %fusion.40 = (f32[2048]{0:T(1024)S(1)}, bf16[2048,768]{0,1:T(8,128)(2,1)S(1)}) fusion(bf16[2048,1792]{1,0:T(8,128)(2,1)} %get-tuple-element.24, bf16[2,1792,768]{2,1,0:T(8,128)(2,1)} %param.15, bf16[1,2048,768]{1,2,0:T(8,128)(2,1)S(1)} %copy.20), kind=kOutput, calls=%fused_computation.73 | convolution fusion | flops 5645006848 | bytes 16392192 | tf_op jit(solution)/shard_map/dot_general | solution.py:10
  63.6 0.0 copy-start.7
  63.6 0.0 copy-start.10
  63.6 1.6 copy-done.7
  65.2 0.0 copy-done.10
  65.2 9.3 %fusion.66 = f32[2048,1792]{1,0:T(8,128)} fusion(bf16[2,768,1792]{2,1,0:T(8,128)(2,1)S(1)} %bitcast.77, bf16[2048,768]{0,1:T(8,128)(2,1)S(1)} %get-tuple-element.27, f32[2048]{0:T(1024)S(1)} %fusion.100), kind=kOutput, calls=%fused_computation.100 | convolution fusion | flops 5641863168 | bytes 20586496 | tf_op jit(solution)/shard_map/jvp()/dot_general | solution.py:22
  74.5 0.0 copy-start.8
  74.5 23.3 %fusion.2 = (bf16[2048,1792]{1,0:T(8,128)(2,1)}, f32[2048,1792]{1,0:T(8,128)}) fusion(f32[2048,1792]{1,0:T(8,128)} %fusion.66, bf16[2048,1792]{1,0:T(8,128)(2,1)} %convolution_convert_fusion.1, bf16[2,768,1792]{2,1,0:T(8,128)(2,1)} %param.13, bf16[2048,768]{0,1:T(8,128)(2,1)} %copy-done.7, f32[2048]{0:T(1024)S(1)} %fusion.100), kind=kOutput, calls=%fused_computation.11 | convolution fusion | flops 5685903360 | bytes 49946624 | tf_op jit(solution)/shard_map/jvp()/dot_general | solution.py:21
  97.9 0.0 copy-done.8
  97.9 0.0 copy-start.14
  97.9 10.8 %fusion.57 = bf16[1,768,1792]{2,1,0:T(8,128)(2,1)} fusion(bf16[2048,1792]{1,0:T(8,128)(2,1)} %get-tuple-element.28, bf16[2048,768]{0,1:T(8,128)(2,1)S(1)} %copy-done.8, f32[2048]{0:T(1024)S(1)} %fusion.100), kind=kOutput, calls=%fused_computation.95 | convolution fusion | flops 5641863168 | bytes 13246464 | tf_op jit(solution)/shard_map/transpose(jvp())/dot_general | solution.py:21
  108.7 0.0 copy-done.14
  108.7 9.2 %convolution_convert_fusion.4 = bf16[2048,768]{0,1:T(8,128)(2,1)} fusion(bf16[2048,1792]{1,0:T(8,128)(2,1)S(1)} %copy-done.14, bf16[2,768,1792]{2,1,0:T(8,128)(2,1)} %param.13), kind=kOutput, calls=%fused_computation.82 | convolution fusion | flops 5637144576 | bytes 13238272 | tf_op jit(solution)/shard_map/transpose(jvp())/dot_general | solution.py:21
  117.8 0.0 copy-done.6
  117.8 14.1 %fusion.61 = bf16[1,1792,768]{2,1,0:T(8,128)(2,1)} fusion(bf16[1,2048,768]{2,1,0:T(8,128)(2,1)S(1)} %copy-done.6, f32[2048,1792]{1,0:T(8,128)} %fusion.66, f32[2048,1792]{1,0:T(8,128)} %get-tuple-element.29), kind=kOutput, calls=%fused_computation.99 | convolution fusion | flops 5660540928 | bytes 35258368 | tf_op jit(solution)/shard_map/transpose(jvp())/dot_general | solution.py:10
  131.9 0.0 copy-done.9
  132.0 12.5 %fusion.60 = bf16[1,768,1792]{2,1,0:T(8,128)(2,1)} fusion(bf16[2048,1792]{1,0:T(8,128)(2,1)} %convolution_convert_fusion.1, bf16[2048,768]{0,1:T(8,128)(2,1)S(1)} %copy-done.9, f32[2048]{0:T(1024)S(1)} %fusion.100, f32[2048,1792]{1,0:T(8,128)} %get-tuple-element.29), kind=kOutput, calls=%fused_computation.98 | convolution fusion | flops 5665259520 | bytes 27926528 | tf_op jit(solution)/shard_map/transpose(jvp())/dot_general | solution.py:22
  144.4 0.0 slice-done.2
  144.4 0.0 slice-done.3
  144.4 0.0 copy-start.11
  144.5 0.0 copy-start.2
  144.5 14.0 %fusion.42 = (f32[2048]{0:T(1024)S(1)}, bf16[2048,768]{0,1:T(8,128)(2,1)}) fusion(bf16[2048,768]{0,1:T(8,128)(2,1)} %copy-done.7, bf16[2048,768]{0,1:T(8,128)(2,1)} %convolution_convert_fusion.4, bf16[2,768,1792]{2,1,0:T(8,128)(2,1)S(1)} %bitcast.79, bf16[2048,1792]{1,0:T(8,128)(2,1)} %convolution_convert_fusion.1, f32[2048,1792]{1,0:T(8,128)} %get-tuple-element.29), kind=kOutput, calls=%fused_computation.75 | convolution fusion | flops 5668599808 | bytes 34217984 | tf_op jit(solution)/shard_map/transpose(jvp())/dot_general | solution.py:22
  158.5 0.0 copy-done.11
  158.5 0.0 copy-done.2
  158.5 0.0 slice-start.4
  158.5 5.2 %fusion.51 = bf16[2048,768]{0,1:T(8,128)(2,1)S(1)} fusion(bf16[2048,768]{0,1:T(8,128)(2,1)} %copy-done.7, bf16[2048,768]{0,1:T(8,128)(2,1)} %get-tuple-element.31, bf16[1,2048,768]{1,2,0:T(8,128)(2,1)S(1)} %copy-done.2, f32[2048]{0:T(1024)S(1)} %multiply_multiply_fusion.3, f32[2048]{0:T(1024)S(1)} %fusion.100), kind=kLoop, calls=%fused_computation.90 | loop fusion | flops 11010048 | bytes 12599296 | tf_op jit(solution)/shard_map/transpose(jvp())/add_any | solution.py:14
  163.7 0.0 slice-start.5
  163.7 9.4 %fusion.58 = bf16[1,1792,768]{2,1,0:T(8,128)(2,1)} fusion(bf16[2048,1792]{1,0:T(8,128)(2,1)} %get-tuple-element.24, bf16[2048,768]{0,1:T(8,128)(2,1)S(1)} %fusion.51), kind=kOutput, calls=%fused_computation.96 | convolution fusion | flops 5638520832 | bytes 13238272 | tf_op jit(solution)/shard_map/transpose(jvp())/dot_general | solution.py:10
  173.1 0.0 slice-done.4
  173.1 0.0 slice-done.5
  173.1 0.0 copy-start.13
  173.1 6.4 %convolution_convert_fusion = bf16[2048,1792]{1,0:T(8,128)(2,1)S(1)} fusion(bf16[2048,768]{0,1:T(8,128)(2,1)S(1)} %fusion.51, bf16[2,1792,768]{2,1,0:T(8,128)(2,1)S(1)} %bitcast.81), kind=kOutput, calls=%fused_computation.65 | convolution fusion | flops 5640814592 | bytes 13238272 | tf_op jit(solution)/shard_map/transpose(jvp())/dot_general | solution.py:10
  179.5 0.0 copy-done.1
  179.5 0.0 copy-done.13
  179.5 0.0 copy-start.15
  179.5 14.2 %fusion.59 = bf16[1,768,1792]{2,1,0:T(8,128)(2,1)} fusion(bf16[2048,1792]{1,0:T(8,128)(2,1)S(1)} %convolution_convert_fusion, bf16[1,2048,768]{1,2,0:T(8,128)(2,1)S(1)} %copy-done.1, f32[2048]{0:T(1024)S(1)} %copy-done.13, f32[2048,1792]{1,0:T(8,128)} %fusion.77), kind=kOutput, calls=%fused_computation.97 | convolution fusion | flops 5665259520 | bytes 27926528 | tf_op jit(solution)/shard_map/transpose(jvp())/dot_general | solution.py:22
  193.7 0.0 copy-done.15
  193.7 17.0 %fusion.54 = bf16[1,768,1792]{2,1,0:T(8,128)(2,1)} fusion(f32[2048,1792]{1,0:T(8,128)} %fusion.77, f32[2048,1792]{1,0:T(8,128)} %get-tuple-element.25, bf16[2048,1792]{1,0:T(8,128)(2,1)} %copy-done.15, bf16[1,2048,768]{1,2,0:T(8,128)(2,1)S(1)} %copy-done.1, f32[2048]{0:T(1024)S(1)} %copy-done.13), kind=kOutput, calls=%fused_computation.94 | convolution fusion | flops 5683609600 | bytes 42606592 | tf_op jit(solution)/shard_map/transpose(jvp())/dot_general | solution.py:21
  210.7 0.1 all-reduce.3.cloned.1.call-update
  210.8 174.8 %all-reduce.3.cloned.1.call-done = (bf16[1,768,1792]{2,1,0:T(8,128)(2,1)}, bf16[1,768,1792]{2,1,0:T(8,128)(2,1)}, bf16[1,768,1792]{2,1,0:T(8,128)(2,1)}, bf16[1,...) async-done(((bf16[1,768,1792]{2,1,0:T(8,128)(2,1)}, bf16[1,768,1792]{2,1,0:T(8,128)(2,1)}, bf16[1,768,1792]{2,1,0:T(8,128)(2,1)}, ...) | async-done | bytes 16515088 | tf_op jit(solution)/shard_map/psum | solution.py:50
  385.6 6.2 %fusion.22 = f32[]{:T(128)} fusion(bf16[1,1792,768]{2,1,0:T(8,128)(2,1)} %get-tuple-element.13, bf16[1,1792,768]{2,1,0:T(8,128)(2,1)} %get-tuple-element.14), kind=kLoop, calls=%fused_computation.46 | loop fusion | flops 11010047 | bytes 5505028 | tf_op jit(solution)/shard_map/reduce_sum | solution.py:52
  391.8 6.0 %fusion.21 = f32[]{:T(128)} fusion(bf16[1,768,1792]{2,1,0:T(8,128)(2,1)} %get-tuple-element.11, bf16[1,768,1792]{2,1,0:T(8,128)(2,1)} %get-tuple-element.12), kind=kLoop, calls=%fused_computation.45 | loop fusion | flops 11010047 | bytes 5505028 | tf_op jit(solution)/shard_map/reduce_sum | solution.py:52
  397.8 0.0 copy-done.3
  397.8 0.0 copy-done.4
  397.8 3.4 fusion.20
  403.3 21.9 %fusion.28 = (bf16[2,1792,768]{2,1,0:T(8,128)(2,1)}, f32[2,1792,768]{2,1,0:T(8,128)}, f32[2,1792,768]{2,1,0:T(8,128)}) fusion(bf16[2,1792,768]{2,1,0:T(8,128)(2,1)} %param.15, f32[]{:T(128)S(6)} %min_shard_map.3, bf16[1,1792,768]{2,1,0:T(8,128)(2,1)} %get-tuple-element.13, bf16[1,1792,768]{2,1,0:T(8,128)(2,1)} %get-tuple-element.14, ...), kind=kLoop, calls=%fused_computation.52 | loop fusion | flops 55050240 | bytes 60555268 | tf_op jit(solution)/shard_map/convert_element_type | solution.py:30
  425.2 37.3 %fusion.19 = (bf16[2,768,1792]{2,1,0:T(8,128)(2,1)}, f32[2,768,1792]{2,1,0:T(8,128)}, f32[2,768,1792]{2,1,0:T(8,128)}, bf16[2,768,1792]{2,1,0:T(8,128)(2,1)}, f3...) fusion(bf16[2,768,1792]{2,1,0:T(8,128)(2,1)} %param.13, f32[]{:T(128)S(6)} %min_shard_map.3, ...), kind=kLoop, calls=%fused_computation.43 | loop fusion | flops 110100480 | bytes 121110528 | tf_op jit(solution)/shard_map/convert_element_type | solution.py:30
  (13 shorter events, 0.0 us)
Async XLA Ops:
  7.2 378.4 %all-reduce.3.cloned.1.call-start = ((), (), s32[]{:S(2)}) async-start(), calls=%async_computation | async-start | bytes 33030144 | tf_op jit(solution)/shard_map/psum | solution.py:50
  10.5 43.4 %copy-start = (bf16[1,2048,768]{1,2,0:T(8,128)(2,1)}, bf16[1,2048,768]{1,2,0:T(8,128)(2,1)S(1)}, u32[]{:S(2)}) copy-start(bf16[1,2048,768]{1,2,0:T(8,128)(2,1)S(1)} %copy.20) | copy-start | bytes 9437188
  11.1 26.5 %copy-start.12 = (f32[2048]{0:T(1024)}, f32[2048]{0:T(1024)S(1)}, u32[]{:S(2)}) copy-start(f32[2048]{0:T(1024)S(1)} %add_rsqrt_fusion) | copy-start | bytes 24580
  16.2 10.4 %copy-start.5 = (bf16[1,2048,768]{2,1,0:T(8,128)(2,1)S(1)}, bf16[1,2048,768]{2,1,0:T(8,128)(2,1)}, u32[]{:S(2)}) copy-start(bf16[1,2048,768]{2,1,0:T(8,128)(2,1)} %param.11) | copy-start | bytes 9437188
  16.2 21.4 %slice-start = ((s8[5505024]{0:T(1024)(128)(4,1)}), s8[4194304]{0:T(1024)(128)(4,1)S(1)}, s32[]{:S(2)}) async-start(s8[5505024]{0:T(1024)(128)(4,1)} %bitcast.76), calls=%async_computation.1 | async-start | bytes 8388608
  26.5 11.1 %slice-start.1 = ((s8[5505024]{0:T(1024)(128)(4,1)}), s8[1310720]{0:T(1024)(128)(4,1)S(1)}, s32[]{:S(2)}) async-start(s8[5505024]{0:T(1024)(128)(4,1)} %bitcast.76), calls=%async_computation.2 | async-start | bytes 2621440
  63.6 1.7 copy-start.7
  63.6 1.7 copy-start.10
  74.5 23.3 %copy-start.8 = (bf16[2048,768]{0,1:T(8,128)(2,1)S(1)}, bf16[2048,768]{0,1:T(8,128)(2,1)}, u32[]{:S(2)}) copy-start(bf16[2048,768]{0,1:T(8,128)(2,1)} %copy-done.7) | copy-start | bytes 9437188
  97.9 10.8 %copy-start.14 = (bf16[2048,1792]{1,0:T(8,128)(2,1)S(1)}, bf16[2048,1792]{1,0:T(8,128)(2,1)}, u32[]{:S(2)}) copy-start(bf16[2048,1792]{1,0:T(8,128)(2,1)} %get-tuple-element.28) | copy-start | bytes 22020100
  108.7 9.2 %copy-start.6 = (bf16[1,2048,768]{2,1,0:T(8,128)(2,1)S(1)}, bf16[1,2048,768]{2,1,0:T(8,128)(2,1)}, u32[]{:S(2)}) copy-start(bf16[1,2048,768]{2,1,0:T(8,128)(2,1)} %param.12) | copy-start | bytes 9437188
  117.8 14.1 %copy-start.9 = (bf16[2048,768]{0,1:T(8,128)(2,1)S(1)}, bf16[2048,768]{0,1:T(8,128)(2,1)}, u32[]{:S(2)}) copy-start(bf16[2048,768]{0,1:T(8,128)(2,1)} %copy-done.7) | copy-start | bytes 9437188
  117.8 26.6 %slice-start.2 = ((s8[5505024]{0:T(1024)(128)(4,1)}), s8[4194304]{0:T(1024)(128)(4,1)S(1)}, s32[]{:S(2)}) async-start(s8[5505024]{0:T(1024)(128)(4,1)} %bitcast.78), calls=%async_computation.3 | async-start | bytes 8388608
  132.0 12.5 %slice-start.3 = ((s8[5505024]{0:T(1024)(128)(4,1)}), s8[1310720]{0:T(1024)(128)(4,1)S(1)}, s32[]{:S(2)}) async-start(s8[5505024]{0:T(1024)(128)(4,1)} %bitcast.78), calls=%async_computation.4 | async-start | bytes 2621440
  144.4 14.0 %copy-start.11 = (f32[2048]{0:T(1024)S(1)}, f32[2048]{0:T(1024)}, u32[]{:S(2)}) copy-start(f32[2048]{0:T(1024)} %copy-done.10) | copy-start | bytes 24580
  144.5 14.0 %copy-start.2 = (bf16[1,2048,768]{1,2,0:T(8,128)(2,1)S(1)}, bf16[1,2048,768]{1,2,0:T(8,128)(2,1)}, u32[]{:S(2)}) copy-start(bf16[1,2048,768]{1,2,0:T(8,128)(2,1)} %copy.21) | copy-start | bytes 9437188
  158.5 14.6 %slice-start.4 = ((s8[5505024]{0:T(1024)(128)(4,1)}), s8[1310720]{0:T(1024)(128)(4,1)S(1)}, s32[]{:S(2)}) async-start(s8[5505024]{0:T(1024)(128)(4,1)} %bitcast.80), calls=%async_computation.5 | async-start | bytes 2621440
  163.7 9.4 %slice-start.5 = ((s8[5505024]{0:T(1024)(128)(4,1)}), s8[4194304]{0:T(1024)(128)(4,1)S(1)}, s32[]{:S(2)}) async-start(s8[5505024]{0:T(1024)(128)(4,1)} %bitcast.80), calls=%async_computation.6 | async-start | bytes 8388608
  173.1 6.4 %copy-start.1 = (bf16[1,2048,768]{1,2,0:T(8,128)(2,1)S(1)}, bf16[1,2048,768]{1,2,0:T(8,128)(2,1)}, u32[]{:S(2)}) copy-start(bf16[1,2048,768]{1,2,0:T(8,128)(2,1)} %copy-done) | copy-start | bytes 9437188
  173.1 6.4 %copy-start.13 = (f32[2048]{0:T(1024)S(1)}, f32[2048]{0:T(1024)}, u32[]{:S(2)}) copy-start(f32[2048]{0:T(1024)} %copy-done.12) | copy-start | bytes 24580
  179.5 14.2 %copy-start.15 = (bf16[2048,1792]{1,0:T(8,128)(2,1)}, bf16[2048,1792]{1,0:T(8,128)(2,1)S(1)}, u32[]{:S(2)}) copy-start(bf16[2048,1792]{1,0:T(8,128)(2,1)S(1)} %convolution_convert_fusion) | copy-start | bytes 22020100
  385.6 12.2 %copy-start.3 = (bf16[1,768,1792]{2,1,0:T(8,128)(2,1)S(1)}, bf16[1,768,1792]{2,1,0:T(8,128)(2,1)}, u32[]{:S(2)}) copy-start(bf16[1,768,1792]{2,1,0:T(8,128)(2,1)} %get-tuple-element.9) | copy-start | bytes 8257540
  385.6 12.2 %copy-start.4 = (bf16[1,768,1792]{2,1,0:T(8,128)(2,1)S(1)}, bf16[1,768,1792]{2,1,0:T(8,128)(2,1)}, u32[]{:S(2)}) copy-start(bf16[1,768,1792]{2,1,0:T(8,128)(2,1)} %get-tuple-element.10) | copy-start | bytes 8257540
Sparse Core Ops, SparseCore 0:
  210.9 174.6 all-reduce.2
where the time goes:
time: 478 us; the launch traced here: 470 us
  matrix products  187 us (39%)
  waiting for transfers between devices  175 us (37%)
  other arithmetic  80.7 us (17%)
  between operations  16.8 us (4%)
  local copies, waits for them, and re-layouts  9.95 us (2%)
    psum x1, waiting for transfers between devices, step(): summed[number] = [lax.psum(by_w[name], 'dp') for name in NAMES]  175 us
    dot_general x5, matrix products, layer(): gate = jnp.dot(a, w['w_gate'], preferred_element_type=jnp.float32)  71.4 us
    dot_general x5, matrix products, layer(): up = jnp.dot(a, w['w_up'], preferred_element_type=jnp.float32)  66.2 us
    convert_element_type x2, other arithmetic, adamw(): return ((w - 0.02 * step).astype(jnp.bfloat16), m, v)  59.2 us
    dot_general x5, matrix products, matmul(): jnp.dot(a, w, preferred_element_type=jnp.float32).astype(jnp.bfloat16)  50 us
    reduce_sum x3, other arithmetic, step(): jnp.sum(g * g)  15.7 us
    unnamed x46, local copies, waits for them, and re-layouts  9.95 us
  transfers between devices with their start and end apart: 1, of which 1 were waited for; matrix products, arithmetic and copies ran while one was open for 0% of the time, Pallas kernels for 0%

commit v1 on v0

v1 whole, which is shorter than its diff:
```python
import functools

import jax
import jax.numpy as jnp
from jax import lax
from jax.experimental import pallas as pl
from jax.experimental.pallas import tpu as pltpu
from jax.sharding import PartitionSpec as P

NAMES = ("w_gate", "w_up", "w_down")
BLOCKS = 8


def matmul(a, w):
    return jnp.dot(a, w, preferred_element_type=jnp.float32).astype(jnp.bfloat16)


def normed(h):
    wide = h.astype(jnp.float32)
    scale = lax.rsqrt(jnp.mean(wide**2, -1, keepdims=True) + 1e-6)
    return (wide * scale).astype(jnp.bfloat16)


def layer(h, w):
    a = normed(h)
    gate = jnp.dot(a, w["w_gate"], preferred_element_type=jnp.float32)
    up = jnp.dot(a, w["w_up"], preferred_element_type=jnp.float32)
    return h + matmul((jax.nn.silu(gate) * up).astype(jnp.bfloat16), w["w_down"])


def adamw_kernel(factor_ref, *refs):
    g, w, m, v = (refs[i : i + 3] for i in (0, 3, 6, 9))
    new_w, new_m, new_v = (refs[len(refs) - 9 :][i : i + 3] for i in (0, 3, 6))
    factor = factor_ref[0]
    for i in range(3):
        grad = g[i][...].astype(jnp.float32) * factor
        mean = 0.9 * m[i][0] + 0.1 * grad
        square = 0.95 * v[i][0] + 0.05 * grad * grad
        wide = w[i][0].astype(jnp.float32)
        new_w[i][0] = (wide - 0.02 * (mean * lax.rsqrt(square + 1e-8) + 0.1 * wide)).astype(jnp.bfloat16)
        new_m[i][0] = mean
        new_v[i][0] = square


def adamw(number, factor, gradients, weights, m, v, so_far):
    whole = [(1, w.shape[1] // BLOCKS, w.shape[2]) for w in weights]
    at_layer = [pl.BlockSpec(s, lambda i: (number, i, 0)) for s in whole]
    alone = [pl.BlockSpec(s[1:], lambda i: (i, 0)) for s in whole]
    carried = [] if so_far is None else list(so_far)
    return pl.pallas_call(
        adamw_kernel,
        grid=(BLOCKS,),
        in_specs=[pl.BlockSpec(memory_space=pltpu.SMEM)] + alone + at_layer * 3 + [pl.BlockSpec(memory_space=pl.ANY)] * len(carried),
        out_specs=at_layer * 3,
        out_shape=[jax.ShapeDtypeStruct(a.shape, a.dtype) for a in (*weights, *m, *v)],
        input_output_aliases={13 + i: i for i in range(len(carried))},
        compiler_params=pltpu.CompilerParams(dimension_semantics=("arbitrary",), vmem_limit_bytes=48 * 2**20),
        cost_estimate=pl.CostEstimate(flops=16 * sum(w.size for w in weights), bytes_accessed=11 * sum(w.size for w in weights), transcendentals=0),
        name=f"adamw_{number}",
    )(factor, *gradients, *weights, *m, *v, *carried)


def solution(mesh):
    def step(x, dy, *arrays):
        weights, m, v = (arrays[i : i + 3] for i in (0, 3, 6))
        layers = weights[0].shape[0]
        h, kept = x[0], []
        for number in range(layers):
            kept.append(h)
            h = layer(h, {name: w[number] for name, w in zip(NAMES, weights, strict=True)})
        by_h, scattered = dy[0], [None] * layers
        before = None
        for number in reversed(range(layers)):
            _, back = jax.vjp(lambda w, h: layer(h, w), {name: w[number] for name, w in zip(NAMES, weights, strict=True)}, kept[number])
            by_w, by_h = back(by_h)
            terms = [by_w[name] for name in NAMES]
            if before is not None:
                terms, _ = lax.optimization_barrier((terms, before))
            before = scattered[number] = [lax.psum_scatter(t, "dp", scatter_dimension=0, tiled=True) for t in terms]
        total = sum(jnp.sum(s.astype(jnp.float32) ** 2) for one in scattered for s in one)
        total = lax.psum(total, "dp")
        count = sum(w.size for w in weights)
        factor = jnp.minimum(1.0, 0.5 * lax.rsqrt(total / count + 1e-30)).reshape(1)
        so_far, before = None, None
        for number in reversed(range(layers)):
            shards = scattered[number]
            if before is not None:
                shards, _ = lax.optimization_barrier((shards, before))
            before = gathered = [lax.all_gather(s, "dp", axis=0, tiled=True) for s in shards]
            so_far = adamw(number, factor, gathered, weights, m, v, so_far)
        return tuple(so_far)

    return jax.shard_map(
        step,
        mesh=mesh,
        in_specs=(P(("rep", "dp"), None, None),) * 2 + (P(None, None, None),) * 9,
        out_specs=(P("rep", None, None),) * 9,
        check_vma=False,
    )
```

time: 478 us -> 497 us (1.040)
  other arithmetic: 80.7 us -> 12.2 us
  Pallas kernels: 0 us -> 59.7 us
  blocking collectives: 0 us -> 16.5 us
  local copies, waits for them, and re-layouts: 9.95 us -> 18.3 us
    psum x1 -> x0, waiting for transfers between devices: 175 us -> none  [step(): summed[number] = [lax.psum(by_w[name], 'dp') for name in NAMES]]
    reduce_scatter x0 -> x6, waiting for transfers between devices: none -> 114 us  [step(): lax.psum_scatter(t, 'dp', scatter_dimension=0, tiled=True)]
    pallas_call x0 -> x2, Pallas kernels: none -> 59.7 us  [adamw(): pl.pallas_call(adamw_kernel, grid=(BLOCKS,), in_specs=[pl.BlockSpec(memor...]
    convert_element_type x2 -> x0, other arithmetic: 59.2 us -> none  [adamw(): return ((w - 0.02 * step).astype(jnp.bfloat16), m, v)]
    all_gather x0 -> x6, waiting for transfers between devices: none -> 55.8 us  [step(): lax.all_gather(s, 'dp', axis=0, tiled=True)]
    psum x0 -> x1, blocking collectives: none -> 16.5 us  [step(): total = lax.psum(total, 'dp')]
    unnamed x46 -> x48, local copies, waits for them, and re-layouts: 9.95 us -> 18.3 us
    reduce_sum x3 -> x6, other arithmetic: 15.7 us -> 7.61 us  [step(): jnp.sum(s.astype(jnp.float32) ** 2)]
  transfers between devices with their start and end apart: 1 -> 12, of which waited for: 1 -> 8; matrix products, arithmetic and copies ran while one was open for 0% -> 23% of each run, Pallas kernels for 0% -> 6%
where the time goes in v1:
time: 497 us; the launch traced here: 489 us
  matrix products  190 us (38%)
  waiting for transfers between devices  173 us (35%)
  Pallas kernels  59.7 us (12%)
  between operations  19.3 us (4%)
  local copies, waits for them, and re-layouts  18.3 us (4%)
  blocking collectives  16.5 us (3%)
  other arithmetic  12.2 us (2%)
    reduce_scatter x6, waiting for transfers between devices, step(): lax.psum_scatter(t, 'dp', scatter_dimension=0, tiled=True)  114 us
    dot_general x5, matrix products, layer(): gate = jnp.dot(a, w['w_gate'], preferred_element_type=jnp.float32)  70.2 us
    dot_general x5, matrix products, layer(): up = jnp.dot(a, w['w_up'], preferred_element_type=jnp.float32)  64.4 us
    pallas_call x2, Pallas kernels, adamw(): pl.pallas_call(adamw_kernel, grid=(BLOCKS,), in_specs=[pl.BlockSpec(memor...  59.7 us
    all_gather x6, waiting for transfers between devices, step(): lax.all_gather(s, 'dp', axis=0, tiled=True)  55.8 us
    dot_general x5, matrix products, matmul(): jnp.dot(a, w, preferred_element_type=jnp.float32).astype(jnp.bfloat16)  55 us
    unnamed x48, local copies, waits for them, and re-layouts  18.3 us
    psum x1, blocking collectives, step(): total = lax.psum(total, 'dp')  16.5 us
  transfers between devices with their start and end apart: 12, of which 8 were waited for; matrix products, arithmetic and copies ran while one was open for 23% of the time, Pallas kernels for 6%

profile of v1, /device:TPU:113, one launch (start us, length us, event | category | flops | bytes accessed | tf_op | source)
XLA Modules:
  0.0 488.9 jit_solution(17980132034237048881)
XLA Ops:
  7.2 0.1 reduce-scatter.11.cloned.1.call-start
  7.3 3.2 copy.29
  10.5 0.7 fusion.15
  11.2 11.6 %convolution_convert_fusion.1 = bf16[2048,1792]{1,0:T(8,128)(2,1)} fusion(bf16[1,2048,768]{2,1,0:T(8,128)(2,1)} %param.12, bf16[2,1792,768]{2,1,0:T(8,128)(2,1)} %refs_5_.3), kind=kOutput, calls=%fused_computation.30 | convolution fusion | flops 5640814592 | bytes 13238272 | tf_op jit(solution)/shard_map/transpose(jvp())/dot_general | solution.py:15
  22.9 9.2 %fusion.46 = f32[2048,1792]{1,0:T(8,128)} fusion(bf16[2,768,1792]{2,1,0:T(8,128)(2,1)S(1)} %bitcast.66, bf16[1,2048,768]{2,1,0:T(8,128)(2,1)S(1)} %copy-done.6, f32[2048]{0:T(1024)S(1)} %add_rsqrt_fusion), kind=kOutput, calls=%fused_computation.66 | convolution fusion | flops 5641863168 | bytes 20586496 | tf_op jit(solution)/shard_map/dot_general | solution.py:26
  32.1 16.2 %multiply_convert_fusion.1 = (bf16[2048,1792]{1,0:T(8,128)(2,1)}, f32[2048,1792]{1,0:T(8,128)}) fusion(f32[2048,1792]{1,0:T(8,128)} %fusion.46, bf16[2,768,1792]{2,1,0:T(8,128)(2,1)S(1)} %bitcast.64, bf16[1,2048,768]{2,1,0:T(8,128)(2,1)} %param.11, f32[2048]{0:T(1024)S(1)} %add_rsqrt_fusion), kind=kOutput, calls=%fused_computation.17 | convolution fusion | flops 5663883264 | bytes 42606592 | tf_op jit(solution)/shard_map/dot_general | solution.py:27
  48.3 9.9 %fusion.19 = (f32[2048]{0:T(1024)S(1)}, bf16[2048,768]{0,1:T(8,128)(2,1)S(1)}) fusion(bf16[2048,1792]{1,0:T(8,128)(2,1)} %get-tuple-element.39, bf16[2,1792,768]{2,1,0:T(8,128)(2,1)} %refs_5_.3, bf16[1,2048,768]{1,2,0:T(8,128)(2,1)S(1)} %copy.29), kind=kOutput, calls=%fused_computation.37 | convolution fusion | flops 5645006848 | bytes 16392192 | tf_op jit(solution)/shard_map/dot_general | solution.py:15
  58.3 1.6 copy-done.8
  59.9 9.2 %fusion.35 = f32[2048,1792]{1,0:T(8,128)} fusion(bf16[2,768,1792]{2,1,0:T(8,128)(2,1)S(1)} %bitcast.64, bf16[2048,768]{0,1:T(8,128)(2,1)S(1)} %get-tuple-element.42, f32[2048]{0:T(1024)S(1)} %fusion.69), kind=kOutput, calls=%fused_computation.55 | convolution fusion | flops 5641863168 | bytes 20586496 | tf_op jit(solution)/shard_map/jvp()/dot_general | solution.py:27
  69.1 23.3 %fusion.2 = (bf16[2048,1792]{1,0:T(8,128)(2,1)}, f32[2048,1792]{1,0:T(8,128)}) fusion(f32[2048,1792]{1,0:T(8,128)} %fusion.35, bf16[2048,1792]{1,0:T(8,128)(2,1)} %convolution_convert_fusion.1, bf16[2,768,1792]{2,1,0:T(8,128)(2,1)} %refs_3_.3, bf16[2048,768]{0,1:T(8,128)(2,1)} %copy-done.8, f32[2048]{0:T(1024)S(1)} %fusion.69), kind=kOutput, calls=%fused_computation.8 | convolution fusion | flops 5685903360 | bytes 49946624 | tf_op jit(solution)/shard_map/jvp()/dot_general | solution.py:26
  92.4 14.2 %fusion.22 = bf16[1792,768]{1,0:T(8,128)(2,1)} fusion(f32[2048,1792]{1,0:T(8,128)} %fusion.35, bf16[1,2048,768]{2,1,0:T(8,128)(2,1)S(1)} %copy-done.7, f32[2048,1792]{1,0:T(8,128)} %get-tuple-element.44), kind=kOutput, calls=%fused_computation.45 | convolution fusion | flops 5660540928 | bytes 35258368 | tf_op jit(solution)/shard_map/transpose(jvp())/dot_general | solution.py:15
  106.6 0.1 reduce-scatter.11.cloned.1.call-update
  106.6 0.1 reduce-scatter.7.cloned.1.call-start
  106.7 10.8 %convolution_convert_fusion.2 = bf16[768,1792]{1,0:T(8,128)(2,1)} fusion(bf16[2048,1792]{1,0:T(8,128)(2,1)} %get-tuple-element.43, bf16[2048,768]{0,1:T(8,128)(2,1)} %copy-done.8, f32[2048]{0:T(1024)S(1)} %fusion.69), kind=kOutput, calls=%fused_computation.41 | convolution fusion | flops 5641863168 | bytes 13246464 | tf_op jit(solution)/shard_map/transpose(jvp())/dot_general | solution.py:26
  117.5 0.1 reduce-scatter.7.cloned.1.call-update
  117.6 0.1 reduce-scatter.9.cloned.1.call-start
  117.7 12.4 %fusion.24 = bf16[768,1792]{1,0:T(8,128)(2,1)} fusion(bf16[2048,1792]{1,0:T(8,128)(2,1)} %convolution_convert_fusion.1, bf16[2048,768]{0,1:T(8,128)(2,1)S(1)} %copy-done.9, f32[2048]{0:T(1024)S(1)} %fusion.69, f32[2048,1792]{1,0:T(8,128)} %get-tuple-element.44), kind=kOutput, calls=%fused_computation.47 | convolution fusion | flops 5665259520 | bytes 27926528 | tf_op jit(solution)/shard_map/transpose(jvp())/dot_general | solution.py:27
  130.1 0.1 reduce-scatter.9.cloned.1.call-update
  130.2 0.1 all-gather.11.cloned.1.call-start
  130.2 3.2 copy.30
  133.4 10.1 %convolution_convert_fusion.4 = bf16[2048,768]{0,1:T(8,128)(2,1)} fusion(bf16[2048,1792]{1,0:T(8,128)(2,1)} %get-tuple-element.43, bf16[2,768,1792]{2,1,0:T(8,128)(2,1)} %refs_3_.3), kind=kOutput, calls=%fused_computation.43 | convolution fusion | flops 5637144576 | bytes 13238272 | tf_op jit(solution)/shard_map/transpose(jvp())/dot_general | solution.py:26
  143.6 0.1 all-gather.11.cloned.1.call-update
  143.6 0.1 all-gather.7.cloned.1.call-start
  143.7 15.2 %fusion.21 = (f32[2048]{0:T(1024)S(1)}, bf16[2048,768]{0,1:T(8,128)(2,1)S(1)}) fusion(bf16[2048,768]{0,1:T(8,128)(2,1)} %copy-done.8, bf16[2048,768]{0,1:T(8,128)(2,1)} %convolution_convert_fusion.4, bf16[2,768,1792]{2,1,0:T(8,128)(2,1)} %refs_4_.3, bf16[2048,1792]{1,0:T(8,128)(2,1)} %convolution_convert_fusion.1, f32[2048,1792]{1,0:T(8,128)} %get-tuple-element.44), kind=kOutput, calls=%fused_computation.39 | convolution fusion | flops 5668599808 | bytes 34217984 | tf_op jit(solution)/shard_map/transpose(jvp())/dot_general | solution.py:27
  158.9 3.9 fusion.30
  162.8 7.6 %reduce-scatter.7.cloned.1.call-done = bf16[96,1792]{1,0:T(8,128)(2,1)} async-done(((bf16[768,1792]{1,0:T(8,128)(2,1)}), bf16[96,1792]{1,0:T(8,128)(2,1)}) %reduce-scatter.7.cloned.1.call-update) | async-done | bytes 344080 | tf_op jit(solution)/shard_map/reduce_scatter | solution.py:79
  170.4 0.1 all-gather.7.cloned.1.call-update
  170.5 0.1 all-gather.9.cloned.1.call-start
  170.6 8.6 %convolution_convert_fusion = bf16[2048,1792]{1,0:T(8,128)(2,1)S(1)} fusion(bf16[2048,768]{0,1:T(8,128)(2,1)} %fusion.30, bf16[2,1792,768]{2,1,0:T(8,128)(2,1)} %refs_5_.3), kind=kOutput, calls=%fused_computation.29 | convolution fusion | flops 5640814592 | bytes 13238272 | tf_op jit(solution)/shard_map/transpose(jvp())/dot_general | solution.py:15
  179.2 3.0 copy-done.18
  182.2 11.5 %fusion.28 = bf16[768,1792]{1,0:T(8,128)(2,1)} fusion(bf16[2048,1792]{1,0:T(8,128)(2,1)S(1)} %convolution_convert_fusion, bf16[1,2048,768]{1,2,0:T(8,128)(2,1)S(1)} %copy-done.5, f32[2048]{0:T(1024)S(1)} %copy-done.17, f32[2048,1792]{1,0:T(8,128)} %fusion.46), kind=kOutput, calls=%fused_computation.49 | convolution fusion | flops 5665259520 | bytes 27926528 | tf_op jit(solution)/shard_map/transpose(jvp())/dot_general | solution.py:27
  193.7 9.5 %reduce-scatter.9.cloned.1.call-done = bf16[96,1792]{1,0:T(8,128)(2,1)} async-done(((bf16[768,1792]{1,0:T(8,128)(2,1)}), bf16[96,1792]{1,0:T(8,128)(2,1)}) %reduce-scatter.9.cloned.1.call-update) | async-done | bytes 344080 | tf_op jit(solution)/shard_map/reduce_scatter | solution.py:79
  203.3 0.1 reduce-scatter.13.cloned.1.call-start
  203.3 10.7 %convolution_convert_fusion.3 = bf16[1792,768]{1,0:T(8,128)(2,1)} fusion(bf16[2048,1792]{1,0:T(8,128)(2,1)} %get-tuple-element.39, bf16[2048,768]{0,1:T(8,128)(2,1)} %fusion.30), kind=kOutput, calls=%fused_computation.42 | convolution fusion | flops 5638520832 | bytes 13238272 | tf_op jit(solution)/shard_map/transpose(jvp())/dot_general | solution.py:15
  214.0 16.7 %fusion.25 = bf16[768,1792]{1,0:T(8,128)(2,1)} fusion(f32[2048,1792]{1,0:T(8,128)} %fusion.46, f32[2048,1792]{1,0:T(8,128)} %get-tuple-element.40, bf16[2048,1792]{1,0:T(8,128)(2,1)} %copy-done.18, bf16[1,2048,768]{1,2,0:T(8,128)(2,1)S(1)} %copy-done.5, f32[2048]{0:T(1024)S(1)} %copy-done.17), kind=kOutput, calls=%fused_computation.48 | convolution fusion | flops 5683609600 | bytes 42606592 | tf_op jit(solution)/shard_map/transpose(jvp())/dot_general | solution.py:26
  230.7 0.1 reduce-scatter.13.cloned.1.call-update
  230.8 0.1 reduce-scatter.15.cloned.1.call-start
  230.8 0.7 reduce-scatter.15.cloned.1.call-update
  231.6 0.1 reduce-scatter.17.cloned.1.call-start
  231.6 0.7 reduce-scatter.17.cloned.1.call-update
  232.4 0.1 all-gather.13.cloned.1.call-start
  232.5 20.8 %all-gather.7.cloned.1.call-done.refs_0_ = bf16[768,1792]{1,0:T(8,128)(2,1)} async-done(((bf16[96,1792]{1,0:T(8,128)(2,1)}), bf16[768,1792]{1,0:T(8,128)(2,1)}) %all-gather.7.cloned.1.call-update) | async-done | bytes 2752528 | tf_op jit(solution)/shard_map/all_gather | solution.py:89
  253.3 24.1 %all-gather.9.cloned.1.call-done.refs_1_ = bf16[768,1792]{1,0:T(8,128)(2,1)} async-done(((bf16[96,1792]{1,0:T(8,128)(2,1)}), bf16[768,1792]{1,0:T(8,128)(2,1)}) %all-gather.9.cloned.1.call-update) | async-done | bytes 2752528 | tf_op jit(solution)/shard_map/all_gather | solution.py:89
  277.4 31.0 %reduce-scatter.13.cloned.1.call-done = bf16[96,1792]{1,0:T(8,128)(2,1)} async-done(((bf16[768,1792]{1,0:T(8,128)(2,1)}), bf16[96,1792]{1,0:T(8,128)(2,1)}) %reduce-scatter.13.cloned.1.call-update) | async-done | bytes 344080 | tf_op jit(solution)/shard_map/reduce_scatter | solution.py:79
  308.4 32.8 %reduce-scatter.15.cloned.1.call-done = bf16[96,1792]{1,0:T(8,128)(2,1)} async-done(((bf16[768,1792]{1,0:T(8,128)(2,1)}), bf16[96,1792]{1,0:T(8,128)(2,1)}) %reduce-scatter.15.cloned.1.call-update) | async-done | bytes 344080 | tf_op jit(solution)/shard_map/reduce_scatter | solution.py:79
  341.2 32.8 %reduce-scatter.17.cloned.1.call-done = bf16[224,768]{1,0:T(8,128)(2,1)} async-done(((bf16[1792,768]{1,0:T(8,128)(2,1)}), bf16[224,768]{1,0:T(8,128)(2,1)}) %reduce-scatter.17.cloned.1.call-update) | async-done | bytes 344080 | tf_op jit(solution)/shard_map/reduce_scatter | solution.py:79
  374.1 0.1 all-gather.15.cloned.1.call-start
  374.1 0.7 all-gather.15.cloned.1.call-update
  374.9 0.1 all-gather.17.cloned.1.call-start
  374.9 0.6 all-gather.17.cloned.1.call-update
  375.5 0.8 multiply_reduce_fusion
  376.3 0.8 multiply_reduce_fusion.2
  377.1 0.8 multiply_reduce_fusion.1
  377.8 1.8 multiply_reduce_fusion.5
  379.6 1.8 multiply_reduce_fusion.4
  382.7 1.8 multiply_reduce_fusion.3
  387.0 16.5 %psum.7 = f32[]{:T(128)} all-reduce(f32[]{:T(128)S(6)} %add.72), channel_id=1, replica_groups=mesh['rep'=2,'dp'=8] {'dp'}, use_global_device_ids=true, to_apply=%region_15.16 | all-reduce | flops 1 | bytes 8 | tf_op jit(solution)/shard_map/psum | solution.py:81
  404.2 1.8 copy-done
  405.9 1.8 copy-done.1
  407.7 29.9 %adamw_1.1 = (bf16[2,768,1792]{2,1,0:T(8,128)(2,1)}, bf16[2,768,1792]{2,1,0:T(8,128)(2,1)}, bf16[2,1792,768]{2,1,0:T(8,128)(2,1)}, f32[2,768,1792]{2,1,0:T(8,128...) custom-call(f32[1]{0:T(128)} %bitcast.9.factor_ref, ...), custom_call_target="tpu_custom_call" | custom-call | flops 132120576 | bytes 90832896 | tf_op jit(solution)/shard_map/adamw_1/pallas_call | solution.py:50
  437.6 10.8 %all-gather.17.cloned.1.call-done.refs_2_ = bf16[1792,768]{1,0:T(8,128)(2,1)} async-done(((bf16[224,768]{1,0:T(8,128)(2,1)}), bf16[1792,768]{1,0:T(8,128)(2,1)}) %all-gather.17.cloned.1.call-update) | async-done | bytes 2752528 | tf_op jit(solution)/shard_map/all_gather | solution.py:89
  448.4 1.8 copy-done.2
  450.2 1.8 copy-done.3
  452.0 29.9 %adamw_0.1 = (bf16[2,768,1792]{2,1,0:T(8,128)(2,1)}, bf16[2,768,1792]{2,1,0:T(8,128)(2,1)}, bf16[2,1792,768]{2,1,0:T(8,128)(2,1)}, f32[2,768,1792]{2,1,0:T(8,128...) custom-call(f32[1]{0:T(128)} %bitcast.9.factor_ref, ...), custom_call_target="tpu_custom_call", output_to_operand_aliasing={{0}: (13, {}), {1}: (14, {}), {2}: (15, {}), {3}: (16, {}),... | custom-call | flops 132120576 | bytes 90832896 | tf_op jit(solution)/shard_map/adamw_0/pallas_call | solution.py:50
  (51 shorter events, 0.3 us)
Async XLA Ops:
  7.2 136.4 %reduce-scatter.11.cloned.1.call-start = ((), (), s32[]{:S(2)}) async-start(), calls=%async_computation.8 | async-start | bytes 3096576 | tf_op jit(solution)/shard_map/reduce_scatter | solution.py:79
  10.5 37.9 %copy-start.4 = (bf16[1,2048,768]{1,2,0:T(8,128)(2,1)}, bf16[1,2048,768]{1,2,0:T(8,128)(2,1)S(1)}, u32[]{:S(2)}) copy-start(bf16[1,2048,768]{1,2,0:T(8,128)(2,1)S(1)} %copy.29) | copy-start | bytes 9437188
  10.5 12.4 %slice-start.2 = ((s8[5505024]{0:T(1024)(128)(4,1)}), s8[4194304]{0:T(1024)(128)(4,1)S(1)}, s32[]{:S(2)}) async-start(s8[5505024]{0:T(1024)(128)(4,1)} %bitcast.65), calls=%async_computation.20 | async-start | bytes 8388608
  11.2 20.9 %copy-start.16 = (f32[2048]{0:T(1024)}, f32[2048]{0:T(1024)S(1)}, u32[]{:S(2)}) copy-start(f32[2048]{0:T(1024)S(1)} %add_rsqrt_fusion) | copy-start | bytes 24580
  11.2 11.7 %slice-start.3 = ((s8[5505024]{0:T(1024)(128)(4,1)}), s8[1310720]{0:T(1024)(128)(4,1)S(1)}, s32[]{:S(2)}) async-start(s8[5505024]{0:T(1024)(128)(4,1)} %bitcast.65), calls=%async_computation.21 | async-start | bytes 2621440
  11.2 11.7 %copy-start.6 = (bf16[1,2048,768]{2,1,0:T(8,128)(2,1)S(1)}, bf16[1,2048,768]{2,1,0:T(8,128)(2,1)}, u32[]{:S(2)}) copy-start(bf16[1,2048,768]{2,1,0:T(8,128)(2,1)} %param.11) | copy-start | bytes 9437188
  11.2 20.9 %slice-start = ((s8[5505024]{0:T(1024)(128)(4,1)}), s8[4194304]{0:T(1024)(128)(4,1)S(1)}, s32[]{:S(2)}) async-start(s8[5505024]{0:T(1024)(128)(4,1)} %bitcast.63), calls=%async_computation.18 | async-start | bytes 8388608
  22.8 9.2 %slice-start.1 = ((s8[5505024]{0:T(1024)(128)(4,1)}), s8[1310720]{0:T(1024)(128)(4,1)S(1)}, s32[]{:S(2)}) async-start(s8[5505024]{0:T(1024)(128)(4,1)} %bitcast.63), calls=%async_computation.19 | async-start | bytes 2621440
  58.3 1.7 copy-start.8
  58.3 1.7 copy-start.14
  69.1 23.3 %copy-start.7 = (bf16[1,2048,768]{2,1,0:T(8,128)(2,1)S(1)}, bf16[1,2048,768]{2,1,0:T(8,128)(2,1)}, u32[]{:S(2)}) copy-start(bf16[1,2048,768]{2,1,0:T(8,128)(2,1)} %param.12) | copy-start | bytes 9437188
  106.6 63.8 %reduce-scatter.7.cloned.1.call-start = ((), (), s32[]{:S(2)}) async-start(), calls=%async_computation.6 | async-start | bytes 3096576 | tf_op jit(solution)/shard_map/reduce_scatter | solution.py:79
  106.7 11.0 %copy-start.9 = (bf16[2048,768]{0,1:T(8,128)(2,1)S(1)}, bf16[2048,768]{0,1:T(8,128)(2,1)}, u32[]{:S(2)}) copy-start(bf16[2048,768]{0,1:T(8,128)(2,1)} %copy-done.8) | copy-start | bytes 9437188
  117.6 85.6 %reduce-scatter.9.cloned.1.call-start = ((), (), s32[]{:S(2)}) async-start(), calls=%async_computation.7 | async-start | bytes 3096576 | tf_op jit(solution)/shard_map/reduce_scatter | solution.py:79
  130.2 102.3 %all-gather.11.cloned.1.call-start = ((), (), s32[]{:S(2)}) async-start(), calls=%async_computation.14 | async-start | bytes 3096576 | tf_op jit(solution)/shard_map/all_gather | solution.py:89
  143.6 15.3 %copy-start.15 = (f32[2048]{0:T(1024)S(1)}, f32[2048]{0:T(1024)}, u32[]{:S(2)}) copy-start(f32[2048]{0:T(1024)} %copy-done.14) | copy-start | bytes 24580
  143.6 109.6 %all-gather.7.cloned.1.call-start = ((), (), s32[]{:S(2)}) async-start(), calls=%async_computation.12 | async-start | bytes 3096576 | tf_op jit(solution)/shard_map/all_gather | solution.py:89
  143.7 15.2 %copy-start.10 = (bf16[2048,768]{0,1:T(8,128)(2,1)S(1)}, bf16[2048,768]{0,1:T(8,128)(2,1)}, u32[]{:S(2)}) copy-start(bf16[2048,768]{0,1:T(8,128)(2,1)} %copy-done.8) | copy-start | bytes 9437188
  170.5 11.7 %copy-start.5 = (bf16[1,2048,768]{1,2,0:T(8,128)(2,1)S(1)}, bf16[1,2048,768]{1,2,0:T(8,128)(2,1)}, u32[]{:S(2)}) copy-start(bf16[1,2048,768]{1,2,0:T(8,128)(2,1)} %copy-done.4) | copy-start | bytes 9437188
  170.5 11.7 %copy-start.17 = (f32[2048]{0:T(1024)S(1)}, f32[2048]{0:T(1024)}, u32[]{:S(2)}) copy-start(f32[2048]{0:T(1024)} %copy-done.16) | copy-start | bytes 24580
  170.5 106.9 %all-gather.9.cloned.1.call-start = ((), (), s32[]{:S(2)}) async-start(), calls=%async_computation.13 | async-start | bytes 3096576 | tf_op jit(solution)/shard_map/all_gather | solution.py:89
  179.2 3.1 copy-start.18
  203.3 105.1 %reduce-scatter.13.cloned.1.call-start = ((), (), s32[]{:S(2)}) async-start(), calls=%async_computation.9 | async-start | bytes 3096576 | tf_op jit(solution)/shard_map/reduce_scatter | solution.py:79
  230.7 144.8 %copy-start.11 = (bf16[224,768]{1,0:T(8,128)(2,1)S(1)}, bf16[224,768]{1,0:T(8,128)(2,1)}, u32[]{:S(2)}) copy-start(bf16[224,768]{1,0:T(8,128)(2,1)} %reduce-scatter.11.cloned.1.call-done) | copy-start | bytes 1032196
  230.7 145.6 %copy-start.12 = (bf16[96,1792]{1,0:T(8,128)(2,1)S(1)}, bf16[96,1792]{1,0:T(8,128)(2,1)}, u32[]{:S(2)}) copy-start(bf16[96,1792]{1,0:T(8,128)(2,1)} %reduce-scatter.7.cloned.1.call-done) | copy-start | bytes 1032196
  230.7 146.4 %copy-start.13 = (bf16[96,1792]{1,0:T(8,128)(2,1)S(1)}, bf16[96,1792]{1,0:T(8,128)(2,1)}, u32[]{:S(2)}) copy-start(bf16[96,1792]{1,0:T(8,128)(2,1)} %reduce-scatter.9.cloned.1.call-done) | copy-start | bytes 1032196
  230.8 110.4 %reduce-scatter.15.cloned.1.call-start = ((), (), s32[]{:S(2)}) async-start(), calls=%async_computation.10 | async-start | bytes 3096576 | tf_op jit(solution)/shard_map/reduce_scatter | solution.py:79
  231.6 142.4 %reduce-scatter.17.cloned.1.call-start = ((), (), s32[]{:S(2)}) async-start(), calls=%async_computation.11 | async-start | bytes 3096576 | tf_op jit(solution)/shard_map/reduce_scatter | solution.py:79
  232.4 205.2 %all-gather.13.cloned.1.call-start = ((), (), s32[]{:S(2)}) async-start(), calls=%async_computation.15 | async-start | bytes 3096576 | tf_op jit(solution)/shard_map/all_gather | solution.py:89
  374.1 63.6 %all-gather.15.cloned.1.call-start = ((), (), s32[]{:S(2)}) async-start(), calls=%async_computation.16 | async-start | bytes 3096576 | tf_op jit(solution)/shard_map/all_gather | solution.py:89
  374.9 73.6 %all-gather.17.cloned.1.call-start = ((), (), s32[]{:S(2)}) async-start(), calls=%async_computation.17 | async-start | bytes 3096576 | tf_op jit(solution)/shard_map/all_gather | solution.py:89
  404.2 1.8 copy-start
  405.9 1.8 copy-start.1
  448.4 1.8 copy-start.2
  450.2 1.8 copy-start.3
Sparse Core Ops, SparseCore 0:
  106.8 30.8 reduce-scatter.10
  140.5 29.8 reduce-scatter.6
  173.3 29.8 reduce-scatter.8
  204.6 24.4 all-gather.10
  230.6 22.6 all-gather.6
  254.7 22.6 all-gather.8
  280.2 28.0 reduce-scatter.12
  311.3 29.8 reduce-scatter.14
  344.1 29.8 reduce-scatter.16
  375.4 24.6 all-gather.12
  401.7 22.5 all-gather.14
  425.7 22.6 all-gather.16

commit v2 on v0

v2 whole, which is shorter than its diff:
```python
import functools

import jax
import jax.numpy as jnp
from jax import lax
from jax.experimental import pallas as pl
from jax.experimental.pallas import tpu as pltpu
from jax.sharding import PartitionSpec as P

CHUNK = 256
TILE = 512
F32, BF16 = jnp.float32, jnp.bfloat16


def dot(a, b, contract):
    return lax.dot_general(a, b, (contract, ((), ())), preferred_element_type=F32)


def scale_of(wide):
    return lax.rsqrt(jnp.mean(wide * wide, -1, keepdims=True) + 1e-6)


def forward_kernel(x_ref, wg_ref, wu_ref, wd_ref, h_ref, hid):
    wide = x_ref[...].astype(F32)
    a = (wide * scale_of(wide)).astype(BF16)
    for at in range(0, hid.shape[1], CHUNK):
        gate = dot(a, wg_ref[0, :, at : at + CHUNK], ((1,), (0,)))
        up = dot(a, wu_ref[0, :, at : at + CHUNK], ((1,), (0,)))
        hid[:, at : at + CHUNK] = (gate * jax.nn.sigmoid(gate) * up).astype(BF16)
    out = dot(hid[...], wd_ref[0], ((1,), (0,))).astype(BF16)
    h_ref[...] = (wide + out.astype(F32)).astype(BF16)


def forward(number, x, wg, wu, wd):
    tokens, d = x.shape
    whole = lambda w: pl.BlockSpec((1, *w.shape[1:]), lambda i: (number, 0, 0))
    rows = pl.BlockSpec((min(TILE, tokens), d), lambda i: (i, 0))
    return pl.pallas_call(
        forward_kernel,
        grid=(tokens // min(TILE, tokens),),
        in_specs=[rows, whole(wg), whole(wu), whole(wd)],
        out_specs=rows,
        out_shape=jax.ShapeDtypeStruct(x.shape, BF16),
        scratch_shapes=[pltpu.VMEM((min(TILE, tokens), wg.shape[2]), BF16)],
        compiler_params=pltpu.CompilerParams(dimension_semantics=("arbitrary",), vmem_limit_bytes=48 * 2**20),
        name="forward",
    )(x, wg, wu, wd)


def train_kernel(
    n, layers, per_layer, comm,
    x_hbm, h_hbm, dy_hbm, wg_hbm, wu_hbm, wd_hbm,
    sum_hbm, norm_hbm,
    h, dy, a, a_t, da, wgu, wd, hid, dgu, g,
    recv_p, recv_1, recv_2, wide_sum, send_1, send_2, red, squares, all_squares,
    load_sem, w_sem, send_sem, recv_sem, keep_sem, norm_send, norm_recv,
):
    tokens, d = h.shape
    tile = min(TILE, tokens)
    tiles = tokens // tile
    chunks = layers * per_layer
    me = lax.axis_index("dp")
    chip, core = me // 2, me % 2
    chips = n // 2
    right = lax.rem(chip + 1, chips) * 2 + core
    left = lax.rem(chip + chips - 1, chips) * 2 + core
    partner = chip * 2 + 1 - core
    half = g.shape[1] // 2
    shard = half // chips
    part = shard // 2
    mine = pl.multiple_of(core * half, 16)
    theirs = pl.multiple_of((1 - core) * half, 16)

    def at_shard(q):
        return pl.multiple_of(lax.rem(chip + q, chips) * shard, 16)

    def remote(src, dst, c, k, to):
        return pltpu.make_async_remote_copy(
            src_ref=src, dst_ref=dst, send_sem=send_sem.at[c, k], recv_sem=recv_sem.at[c, k],
            device_id={"dp": to}, device_id_type=pl.DeviceIdType.MESH,
        )

    def load_weights(it, slot):
        layer, j = layers - 1 - it // per_layer, lax.rem(it, per_layer)
        columns = pl.ds(pl.multiple_of(j * CHUNK, CHUNK), CHUNK)
        return (
            pltpu.make_async_copy(wg_hbm.at[layer, :, columns], wgu.at[slot, :, pl.ds(0, CHUNK)], w_sem.at[slot, 0]),
            pltpu.make_async_copy(wu_hbm.at[layer, :, columns], wgu.at[slot, :, pl.ds(CHUNK, CHUNK)], w_sem.at[slot, 1]),
            pltpu.make_async_copy(wd_hbm.at[layer, columns, :], wd.at[slot], w_sem.at[slot, 2]),
        )

    def pair(c, slot):
        return remote(g.at[slot, pl.ds(theirs, half)], recv_p.at[c], c, 0, partner)

    def first(c, slot, k):
        return remote(send_1.at[slot, k], recv_1.at[c, k], c, 1 + k, (right, left)[k])

    def second(c, slot, k):
        return remote(send_2.at[slot, k], recv_2.at[c, k], c, 3 + k, (right, left)[k])

    def spread(c, slot, k):
        rows = pl.ds(mine + at_shard(0), shard)
        return remote(red.at[slot], sum_hbm.at[c, rows], c, 5 + k, (right, left)[k])

    def keep(c, slot):
        return pltpu.make_async_copy(red.at[slot], sum_hbm.at[c, pl.ds(mine + at_shard(0), shard)], keep_sem.at[c])

    def forward_on(c, k):
        rows = pl.ds(mine + at_shard((chips - 1, 1)[k]) + k * part, part)
        return remote(sum_hbm.at[c, rows], sum_hbm.at[c, rows], c, 7 + k, (right, left)[k])

    def pair_back(c):
        rows = pl.ds(mine, half)
        return remote(sum_hbm.at[c, rows], sum_hbm.at[c, rows], c, 9, partner)

    others = [lax.rem(me + k, n) for k in range(1, n)]
    if comm:
        barrier = pltpu.get_barrier_semaphore()
        for other in others:
            pl.semaphore_signal(barrier, inc=1, device_id={"dp": other}, device_id_type=pl.DeviceIdType.MESH)

    loads = [pltpu.make_async_copy(src, dst, load_sem.at[i]) for i, (src, dst) in enumerate([(h_hbm, h), (dy_hbm, dy)])]
    for load in loads:
        load.start()
    for load in load_weights(0, 0):
        load.start()
    squares[...] = jnp.zeros_like(squares)
    if comm:
        pl.semaphore_wait(barrier, n - 1)
    loads[0].wait()

    def prepare():
        def body(t, _):
            rows = pl.ds(pl.multiple_of(t * tile, tile), tile)
            wide = h[rows, :].astype(F32)
            normed = (wide * scale_of(wide)).astype(BF16)
            a[rows, :] = normed
            a_t[:, rows] = normed.T
            return 0

        lax.fori_loop(0, tiles, body, 0)

    prepare()
    da[...] = jnp.zeros_like(da)
    loads[1].wait()

    def next_layer():
        def body(t, _):
            rows = pl.ds(pl.multiple_of(t * tile, tile), tile)
            wide, by_a = h[rows, :].astype(F32), da[rows, :].astype(BF16).astype(F32)
            scale = scale_of(wide)
            inner = jnp.sum(by_a * wide, -1, keepdims=True)
            by_h = (by_a * scale - wide * (scale * scale * scale * inner * (1.0 / d))).astype(BF16)
            dy[rows, :] = (dy[rows, :].astype(F32) + by_h.astype(F32)).astype(BF16)
            return 0

        lax.fori_loop(0, tiles, body, 0)
        load = pltpu.make_async_copy(x_hbm, h, load_sem.at[0])
        load.start()
        load.wait()
        prepare()

    def compute(it):
        slot = lax.rem(it, 2)
        for load in load_weights(it, slot):
            load.wait()

        @pl.when(it + 1 < chunks)
        def _():
            for load in load_weights(it + 1, 1 - slot):
                load.start()

        def body(t, _):
            rows = pl.ds(pl.multiple_of(t * tile, tile), tile)
            both = dot(a[rows, :], wgu[slot], ((1,), (0,)))
            by_hid = dot(dy[rows, :], wd[slot], ((1,), (1,))).astype(BF16).astype(F32)
            gate, up = both[:, :CHUNK], both[:, CHUNK:]
            sig = jax.nn.sigmoid(gate)
            act = gate * sig
            hid[rows, :] = (act * up).astype(BF16)
            dgu[rows, :CHUNK] = (by_hid * up * (sig + act * (1.0 - sig))).astype(BF16)
            dgu[rows, CHUNK:] = (by_hid * act).astype(BF16)

            @pl.when(it < (layers - 1) * per_layer)
            def _():
                da[rows, :] += dot(dgu[rows, :], wgu[slot], ((1,), (1,)))

            return 0

        lax.fori_loop(0, tiles, body, 0)
        by_wd = dot(hid[...], dy[...], ((0,), (0,))).astype(BF16)
        for k in range(d // CHUNK):
            g[slot, 2 * d + k * CHUNK : 2 * d + (k + 1) * CHUNK, :] = by_wd[:, k * CHUNK : (k + 1) * CHUNK]
        by_wgu = dot(a_t[...], dgu[...], ((1,), (0,))).astype(BF16)
        g[slot, :d, :] = by_wgu[:, :CHUNK]
        g[slot, d : 2 * d, :] = by_wgu[:, CHUNK:]

    def within(c, act):
        pl.when((c >= 0) & (c < chunks))(act)

    def serve(it):
        def last():
            c = it - 6
            pair_back(c).wait()

        within(it - 6, last)

        def five():
            c = it - 5
            for k in range(2):
                forward_on(c, k).wait()
            pair_back(c).start()

        within(it - 5, five)

        def four():
            c = it - 4
            keep(c, lax.rem(c, 2)).wait()
            for k in range(2):
                spread(c, lax.rem(c, 2), k).wait()
            for k in range(2):
                forward_on(c, k).start()

        within(it - 4, four)

        def three():
            c = it - 3
            for k in range(2):
                second(c, lax.rem(c, 2), k).wait()
            total = wide_sum[lax.rem(c, 3), pl.ds(at_shard(0), shard), :]
            total = (total + recv_2[c, 0].astype(F32) + recv_2[c, 1].astype(F32)).astype(BF16)
            red[lax.rem(c, 2)] = total
            spread(c, lax.rem(c, 2), 0).start()
            spread(c, lax.rem(c, 2), 1).start()
            keep(c, lax.rem(c, 2)).start()
            total = total.astype(F32)
            squares[...] += jnp.sum((total * total).reshape(shard // 8, 8, CHUNK), 0)

        within(it - 3, three)

        def two():
            c = it - 2
            for k in range(2):
                first(c, lax.rem(c, 2), k).wait()
            for k, q in enumerate((1, chips - 1)):
                rows = wide_sum[lax.rem(c, 3), pl.ds(at_shard(q), shard), :]
                extra = recv_1[c, k].astype(F32)
                send_2[lax.rem(c, 2), k, k * part : (k + 1) * part] = (rows[k * part : (k + 1) * part] + extra).astype(BF16)
                send_2[lax.rem(c, 2), k, (1 - k) * part : (2 - k) * part] = rows[(1 - k) * part : (2 - k) * part].astype(BF16)
                second(c, lax.rem(c, 2), k).start()

        within(it - 2, two)

        def one():
            c = it - 1
            pair(c, lax.rem(c, 2)).wait()
            wide_sum[lax.rem(c, 3)] = g[lax.rem(c, 2), pl.ds(mine, half), :].astype(F32) + recv_p[c].astype(F32)
            for k in range(2):
                send_1[lax.rem(c, 2), k] = wide_sum[lax.rem(c, 3), pl.ds(at_shard(2) + k * part, part), :].astype(BF16)
                first(c, lax.rem(c, 2), k).start()

        within(it - 1, one)

    def step(it, _):
        if comm:
            serve(it)
        pl.when(it == (layers - 1) * per_layer)(next_layer)
        pl.when(it < chunks)(lambda: compute(it))
        if comm:
            pl.when(it < chunks)(lambda: pair(it, lax.rem(it, 2)).start())
        return 0

    lax.fori_loop(0, chunks + 7 if comm else chunks, step, 0)

    if comm:
        all_squares[pl.ds(me, 1)] = squares[...][None]
        sends = [
            pltpu.make_async_remote_copy(
                src_ref=squares, dst_ref=all_squares.at[me], send_sem=norm_send.at[k], recv_sem=norm_recv.at[k],
                device_id={"dp": other}, device_id_type=pl.DeviceIdType.MESH,
            )
            for k, other in enumerate(others)
        ]
        for send in sends:
            send.start()
        for send in sends:
            send.wait()
        total = all_squares[0]
        for k in range(1, n):
            total += all_squares[k]
        norm_hbm[...] = total
    else:
        norm_hbm[...] = squares[...]
        pltpu.sync_copy(g.at[0], sum_hbm.at[0])


def train(n, x, h, dy, wg, wu, wd, comm=True):
    tokens, d = x.shape
    layers, _, ff = wg.shape
    per_layer = ff // CHUNK
    chunks, rows = layers * per_layer, 3 * d
    half = rows // 2
    shard = half // (n // 2)
    part = shard // 2
    hbm = pl.BlockSpec(memory_space=pl.ANY)
    vmem = pltpu.VMEM
    dma = pltpu.SemaphoreType.DMA
    return pl.pallas_call(
        functools.partial(train_kernel, n, layers, per_layer, comm),
        in_specs=[hbm] * 6,
        out_specs=[hbm, pl.BlockSpec(memory_space=pltpu.VMEM)],
        out_shape=[jax.ShapeDtypeStruct((chunks, rows, CHUNK), BF16), jax.ShapeDtypeStruct((8, CHUNK), F32)],
        scratch_shapes=[
            vmem((tokens, d), BF16), vmem((tokens, d), BF16), vmem((tokens, d), BF16), vmem((d, tokens), BF16), vmem((tokens, d), F32),
            vmem((2, d, 2 * CHUNK), BF16), vmem((2, CHUNK, d), BF16), vmem((tokens, CHUNK), BF16), vmem((tokens, 2 * CHUNK), BF16),
            vmem((2, rows, CHUNK), BF16),
            vmem((chunks, half, CHUNK), BF16), vmem((chunks, 2, part, CHUNK), BF16), vmem((chunks, 2, shard, CHUNK), BF16),
            vmem((3, half, CHUNK), F32), vmem((2, 2, part, CHUNK), BF16), vmem((2, 2, shard, CHUNK), BF16), vmem((2, shard, CHUNK), BF16),
            vmem((8, CHUNK), F32), vmem((n, 8, CHUNK), F32),
            dma((2,)), dma((2, 3)), dma((chunks, 10)), dma((chunks, 10)), dma((chunks,)), dma((n - 1,)), dma((n - 1,)),
        ],
        compiler_params=pltpu.CompilerParams(collective_id=0 if comm else None, has_side_effects=True, vmem_limit_bytes=63 * 2**20),
        cost_estimate=pl.CostEstimate(flops=14 * tokens * d * ff * layers, bytes_accessed=60 * 2**20, transcendentals=0),
        name="train",
    )(x, h, dy, wg, wu, wd)


def adamw_kernel(count, squares_ref, g_ref, *refs):
    w, m, v, new_w, new_m, new_v = (refs[i : i + 3] for i in range(0, 18, 3))
    total = jnp.sum(squares_ref[...], (0, 1), keepdims=True)
    factor = jnp.minimum(1.0, 0.5 * lax.rsqrt(total / count + 1e-30))
    d = w[0].shape[1]
    for i in range(3):
        if i < 2:
            grad = g_ref[0, i * d : (i + 1) * d, :]
        else:
            grad = jnp.concatenate([g_ref[0, 2 * d + k : 2 * d + k + CHUNK, :] for k in range(0, d, CHUNK)], 1)
        grad = grad.astype(F32) * factor
        mean = 0.9 * m[i][0] + 0.1 * grad
        square = 0.95 * v[i][0] + 0.05 * grad * grad
        wide = w[i][0].astype(F32)
        new_w[i][0] = (wide - 0.02 * (mean * lax.rsqrt(square + 1e-8) + 0.1 * wide)).astype(BF16)
        new_m[i][0] = mean
        new_v[i][0] = square


def adamw(squares, g, weights, m, v):
    layers, d, ff = weights[0].shape
    per_layer = ff // CHUNK
    across = pl.BlockSpec((1, d, CHUNK), lambda i: (layers - 1 - i // per_layer, 0, i % per_layer))
    down = pl.BlockSpec((1, CHUNK, d), lambda i: (layers - 1 - i // per_layer, i % per_layer, 0))
    each = [across, across, down] * 3
    count = sum(w.size for w in weights)
    return pl.pallas_call(
        functools.partial(adamw_kernel, count),
        grid=(layers * per_layer,),
        in_specs=[pl.BlockSpec((8, CHUNK), lambda i: (0, 0)), pl.BlockSpec((1, 3 * d, CHUNK), lambda i: (i, 0, 0))] + each,
        out_specs=each,
        out_shape=[jax.ShapeDtypeStruct(t.shape, t.dtype) for t in (*weights, *m, *v)],
        compiler_params=pltpu.CompilerParams(dimension_semantics=("arbitrary",), vmem_limit_bytes=48 * 2**20),
        cost_estimate=pl.CostEstimate(flops=16 * count, bytes_accessed=22 * count, transcendentals=0),
        name="adamw",
    )(squares, g, *weights, *m, *v)


def solution(mesh):
    n = mesh.shape["dp"]

    def step(x, dy, *arrays):
        weights, m, v = (arrays[i : i + 3] for i in (0, 3, 6))
        h = forward(0, x[0], *weights)
        g, squares = train(n, x[0], h, dy[0], *weights)
        return tuple(adamw(squares, g, weights, m, v))

    return jax.shard_map(
        step,
        mesh=mesh,
        in_specs=(P(("rep", "dp"), None, None),) * 2 + (P(None, None, None),) * 9,
        out_specs=(P("rep", None, None),) * 9,
        check_vma=False,
    )
```

time: 478 us -> 275 us (0.58); the launches traced: 470 us -> 275 us
  Pallas kernels: 0 us -> 269 us
  matrix products: 187 us -> 0 us
  waiting for transfers between devices: 175 us -> 0 us
  other arithmetic: 80.7 us -> 0 us
  between operations: 16.8 us -> 0.84 us
  local copies, waits for them, and re-layouts: 9.95 us -> 4.91 us
    pallas_call x0 -> x3, Pallas kernels: none -> 269 us  [the longest x1 187 us: train(): pl.pallas_call(functools.partial(train_kernel, n, layers, per_layer, comm...]
    dot_general x15 -> x0, matrix products: 187 us -> none  [the longest x5 71.4 us: layer(): gate = jnp.dot(a, w['w_gate'], preferred_element_type=jnp.float32)]
    psum x1 -> x0, waiting for transfers between devices: 175 us -> none  [step(): summed[number] = [lax.psum(by_w[name], 'dp') for name in NAMES]]
    convert_element_type x2 -> x0, other arithmetic: 59.2 us -> none  [adamw(): return ((w - 0.02 * step).astype(jnp.bfloat16), m, v)]
    reduce_sum x4 -> x0, other arithmetic: 16.3 us -> none  [the longest x3 15.7 us: step(): jnp.sum(g * g)]
    add_any x1 -> x0, other arithmetic: 5.15 us -> none  [normed(): wide = h.astype(jnp.float32)]
    unnamed x46 -> x6, local copies, waits for them, and re-layouts: 9.95 us -> 4.91 us
  transfers between devices with their start and end apart: 1 -> 0, of which waited for: 1 -> 0; matrix products, arithmetic and copies ran while one was open for 0% -> 0% of each run, Pallas kernels for 0% -> 0%
where the time goes in v2:
time: 275 us
  Pallas kernels  269 us (98%)
  local copies, waits for them, and re-layouts  4.91 us (2%)
    pallas_call x1, Pallas kernels, train(): pl.pallas_call(functools.partial(train_kernel, n, layers, per_layer, comm...  187 us
    pallas_call x1, Pallas kernels, adamw(): pl.pallas_call(functools.partial(adamw_kernel, count), grid=(layers * per...  59.1 us
    pallas_call x1, Pallas kernels, forward(): pl.pallas_call(forward_kernel, grid=(tokens // min(TILE, tokens),), in_sp...  22.5 us

profile of v2, /device:TPU:113, one launch (start us, length us, event | category | flops | bytes accessed | tf_op | source)
XLA Modules:
  0.0 274.5 jit_solution(12250517972927432056)
XLA Ops:
  0.6 22.5 %forward.1.h_hbm = bf16[2048,768]{1,0:T(8,128)(2,1)S(1)} custom-call(bf16[2048,768]{1,0:T(8,128)(2,1)} %bitcast.2, bf16[2,768,1792]{2,1,0:T(8,128)(2,1)} %refs_0_.1, bf16[2,768,1792]{2,1,0:T(8,128)(2,1)} %refs_1_.1, bf16[2,1792,768]{2,1,0:T(8,128)(2,1)} %refs_2_.1), custom_call_target="tpu_custom_call" | custom-call | tf_op jit(solution)/shard_map/forward/pallas_call | solution.py:38
  23.1 0.0 copy-start.1
  23.1 1.7 copy-done.1
  24.8 187.2 %train.1 = (bf16[14,2304,256]{2,1,0:T(8,128)(2,1)}, f32[8,256]{1,0:T(8,128)}) custom-call(bf16[2048,768]{1,0:T(8,128)(2,1)} %bitcast.3, bf16[2048,768]{1,0:T(8,128)(2,1)} %copy-done.1, bf16[2048,768]{1,0:T(8,128)(2,1)} %bitcast.4, bf16[2,768,1792]{2,1,0:T(8,128)(2,1)} %refs_0_.1, bf16[2,768,1792]{2,1,0:T(8,128)(2,1)} %refs_1_.1, bf16[2,1792,768]{2,1,0:T(8,128)(2,1)} %refs_2_.1), custom_call_target="tpu_custom_call" | custom-call | flops 78920024064 | bytes 62914560 | tf_op jit(solution)/shard_map/train/pallas_call | solution.py:308
  212.0 0.0 copy-start
  212.0 2.6 copy-done
  214.6 0.0 copy-start.2
  214.6 0.7 copy-done.2
  215.3 59.1 %adamw.1 = (bf16[2,768,1792]{2,1,0:T(8,128)(2,1)}, bf16[2,768,1792]{2,1,0:T(8,128)(2,1)}, bf16[2,1792,768]{2,1,0:T(8,128)(2,1)}, f32[2,768,1792]{2,1,0:T(8,128)}...) custom-call(f32[8,256]{1,0:T(8,128)S(1)} %copy-done.2, ...), custom_call_target="tpu_custom_call" | custom-call | flops 132120576 | bytes 181665792 | tf_op jit(solution)/shard_map/adamw/pallas_call | solution.py:354
Async XLA Ops:
  23.1 1.7 copy-start.1
  212.0 2.6 copy-start
  214.6 0.7 copy-start.2
